TPU v7x, 32 devices: a whole 2x2x4 slice. The times are simulated.
32 devices in a mesh: dp: 8 (over y, x, core), tensor: 4 (over z).
Axes of the slice: x: 2, y: 2, z: 4, core: 2. Of those that a mesh axis runs over, the one named last changes fastest.
Arguments:
- layer_input: float32 [16, 512, 2048], P('dp', 'tensor'), may hold values from -6 to 6
- segments: int32 [16, 512], P('dp'), may hold values from 0 to 7, never falling along the last dimension, each value on 1 to 256 neighbouring positions
- gain_attn: bfloat16 [2048], P('dp'), may hold values from 0.5 to 1.5
- w_qkv: bfloat16 [2048, 4, 640], P('dp', 'tensor'), as said below
- w_out_t: bfloat16 [2048, 2048], P('dp', 'tensor'), may hold values from -0.75 to 0.75
- gain_mlp: bfloat16 [2048], P('dp'), may hold values from 0.5 to 1.5
- w_gate_up: bfloat16 [2048, 2, 5632], P('dp', None, 'tensor'), may hold values from -0.125 to 0.125
- w_down_t: bfloat16 [2048, 5632], P('dp', 'tensor'), may hold values from -0.078125 to 0.078125
- cotangent: float32 [16, 512, 2048], P('dp', 'tensor'), may hold values from -6 to 6
Outputs:
- output: float32 [16, 512, 2048], P('dp', 'tensor')
- input_grad: float32 [16, 512, 2048], P('dp', 'tensor')
- gain_attn_grad: float32 [2048], P('dp')
- qkv_grad: float32 [2048, 4, 640], P('dp', 'tensor')
- out_grad: float32 [2048, 2048], P('dp', 'tensor')
- gain_mlp_grad: float32 [2048], P('dp')
- gate_up_grad: float32 [2048, 2, 5632], P('dp', None, 'tensor')
- down_grad: float32 [2048, 5632], P('dp', 'tensor')
Inputs may be any that keep to these rules, and one draw needn't show every extreme that they name: `w_qkv`: for each key-value group the columns hold the queries of its 8 heads, then its key, then its value.
All inputs are finite; a program needn't handle non-finite values.
Results may differ from a plain program's by a relative error of at most 0.013.
Values may be sent and summed in bfloat16 or wider, within the bound.
A program may use at most 256 MiB of HBM per device.

v0:
```python
import math
import jax
import jax.numpy as jnp
from jax import lax
from jax.sharding import PartitionSpec as P

H = 32
KV = 4
HD = 64
NORM_EPS = 1e-05


def rope_tables(segment_row, head_size):
    row_count = segment_row.shape[0]
    earlier = jnp.sum((segment_row[None, :] < segment_row[:, None]).astype(jnp.int32), axis=1)
    position = (jnp.arange(row_count, dtype=jnp.int32) - earlier).astype(jnp.float32)
    half_size = head_size // 2
    frequency = jnp.exp(
        jnp.arange(half_size, dtype=jnp.float32) * (-2.0 * math.log(10000.0) / head_size)
    )
    angles = position[:, None] * frequency[None, :]
    return (jnp.cos(angles), jnp.sin(angles))


def expand_table(angle_table, rank_count):
    return angle_table.reshape(
        (angle_table.shape[0],) + (1,) * (rank_count - 2) + (angle_table.shape[1],)
    )


def rotate(values, cosine, sine_tab):
    half_size = values.shape[-1] // 2
    cosine = expand_table(cosine, values.ndim)
    sine_tab = expand_table(sine_tab, values.ndim)
    first_half = values[..., :half_size]
    second_half = values[..., half_size:]
    return jnp.concatenate(
        [
            first_half * cosine - second_half * sine_tab,
            second_half * cosine + first_half * sine_tab,
        ],
        axis=-1,
    )


def unrotate(values, cosine, sine_tab):
    half_size = values.shape[-1] // 2
    cosine = expand_table(cosine, values.ndim)
    sine_tab = expand_table(sine_tab, values.ndim)
    first_half = values[..., :half_size]
    second_half = values[..., half_size:]
    return jnp.concatenate(
        [
            first_half * cosine + second_half * sine_tab,
            second_half * cosine - first_half * sine_tab,
        ],
        axis=-1,
    )


def allowed_pairs(segment_row):
    row_count = segment_row.shape[0]
    position = jnp.arange(row_count, dtype=jnp.int32)
    return (segment_row[:, None] == segment_row[None, :]) & (position[None, :] <= position[:, None])


def norm_forward(row_block, gain_row):
    inv_rms = lax.rsqrt(jnp.mean(row_block * row_block, axis=-1, keepdims=True) + NORM_EPS)
    return ((row_block * inv_rms * gain_row.astype(jnp.float32)).astype(jnp.bfloat16), inv_rms)


def norm_backward(row_block, inv_rms, gain_row, upstream):
    weighted = upstream * gain_row.astype(jnp.float32)
    back_term = inv_rms * weighted - row_block * (inv_rms * inv_rms * inv_rms) * jnp.mean(
        weighted * row_block, axis=-1, keepdims=True
    )
    return (back_term, jnp.sum(upstream * row_block * inv_rms, axis=0))


def split_heads(qkv_rows, head_group, head_size):
    row_count, groups = (qkv_rows.shape[0], qkv_rows.shape[1])
    query = qkv_rows[:, :, : head_group * head_size].reshape(
        row_count, groups, head_group, head_size
    )
    key_part = qkv_rows[:, :, head_group * head_size : (head_group + 1) * head_size]
    value_part = qkv_rows[:, :, (head_group + 1) * head_size :]
    return (query, key_part, value_part)


def score_block(query, key_part, allowed, head_size):
    scores = jnp.einsum("igne,jge->gnij", query, key_part, preferred_element_type=jnp.float32) * (
        1.0 / math.sqrt(head_size)
    )
    return jnp.where(allowed[None, None], scores, jnp.float32(-1e30))


def attend_forward(qkv_rows, segment_row, head_group, head_size):
    cosine, sine_tab = rope_tables(segment_row, head_size)
    query, key_part, value_part = split_heads(qkv_rows, head_group, head_size)
    query = rotate(query, cosine, sine_tab).astype(jnp.bfloat16)
    key_part = rotate(key_part, cosine, sine_tab).astype(jnp.bfloat16)
    value_part = value_part.astype(jnp.bfloat16)
    allowed = allowed_pairs(segment_row)
    scores = score_block(query, key_part, allowed, head_size)
    row_max = jnp.max(scores, axis=-1, keepdims=True)
    log_total = row_max + jnp.log(jnp.sum(jnp.exp(scores - row_max), axis=-1, keepdims=True))
    weights = jnp.exp(scores - log_total).astype(jnp.bfloat16)
    mixed = jnp.einsum("gnij,jge->igne", weights, value_part, preferred_element_type=jnp.float32)
    mixed = mixed.astype(jnp.bfloat16).reshape(qkv_rows.shape[0], -1)
    return (mixed, (query, key_part, value_part, log_total, cosine, sine_tab, allowed))


def attend_backward(grad_out, saved, head_size):
    query, key_part, value_part, log_total, cosine, sine_tab, allowed = saved
    row_count, groups, head_group = (query.shape[0], query.shape[1], query.shape[2])
    scores = score_block(query, key_part, allowed, head_size)
    weights = jnp.exp(scores - log_total)
    grad_heads = grad_out.reshape(row_count, groups, head_group, head_size)
    grad_value = jnp.einsum(
        "gnij,igne->jge",
        weights.astype(jnp.bfloat16),
        grad_heads,
        preferred_element_type=jnp.float32,
    )
    grad_weights = jnp.einsum(
        "igne,jge->gnij", grad_heads, value_part, preferred_element_type=jnp.float32
    )
    grad_scores = (
        weights
        * (grad_weights - jnp.sum(weights * grad_weights, axis=-1, keepdims=True))
        * (1.0 / math.sqrt(head_size))
    )
    grad_scores = grad_scores.astype(jnp.bfloat16)
    grad_query = jnp.einsum(
        "gnij,jge->igne", grad_scores, key_part, preferred_element_type=jnp.float32
    )
    grad_key = jnp.einsum("gnij,igne->jge", grad_scores, query, preferred_element_type=jnp.float32)
    grad_query = unrotate(grad_query, cosine, sine_tab).reshape(
        row_count, groups, head_group * head_size
    )
    grad_key = unrotate(grad_key, cosine, sine_tab)
    return jnp.concatenate([grad_query, grad_key, grad_value], axis=2).astype(jnp.bfloat16)


def outer_product(left_rows, right_rows):
    return lax.dot_general(
        left_rows, right_rows, (((0,), (0,)), ((), ())), preferred_element_type=jnp.float32
    )


def right_product(left_rows, right_matrix):
    return lax.dot_general(
        left_rows, right_matrix, (((1,), (1,)), ((), ())), preferred_element_type=jnp.float32
    )


def spread_forward(row_block):
    return lax.all_gather(row_block, "tensor", axis=0, tiled=True)


def spread_backward(row_block):
    return lax.all_gather(row_block, "tensor", axis=0, tiled=True)


def branch_sum(term_fn, local_rows):
    return lax.psum_scatter(
        term_fn(jnp.int32(0), lax.axis_size("tensor") * local_rows),
        "tensor",
        scatter_dimension=0,
        tiled=True,
    )


def input_sum(term_fn, local_rows):
    return lax.psum_scatter(
        term_fn(jnp.int32(0), lax.axis_size("tensor") * local_rows),
        "tensor",
        scatter_dimension=0,
        tiled=True,
    )


def add_terms(left_terms, right_terms):
    if left_terms is None:
        return right_terms
    return tuple((left_term + right_term for left_term, right_term in zip(left_terms, right_terms)))


def body(
    layer_input, segments, gain_attn, w_qkv, w_out_t, gain_mlp, w_gate_up, w_down_t, cotangent
):
    head_group = H // KV
    weight_shard = (gain_attn, w_qkv, w_out_t, gain_mlp, w_gate_up, w_down_t)
    local_rows = layer_input.shape[1]
    outputs = []
    input_grads = []
    grad_total = None
    owned_grads = None
    for number in range(layer_input.shape[0]):
        gathered_weights = (
            lax.all_gather(weight_shard[0], "dp", axis=0, tiled=True),
            lax.all_gather(weight_shard[1], "dp", axis=0, tiled=True),
            lax.all_gather(weight_shard[2], "dp", axis=0, tiled=True),
            lax.all_gather(weight_shard[3], "dp", axis=0, tiled=True),
            lax.all_gather(weight_shard[4], "dp", axis=0, tiled=True),
            lax.all_gather(weight_shard[5], "dp", axis=0, tiled=True),
        )
        g_attn, qkv_w, out_w, g_mlp, gu_w, down_w = gathered_weights
        model_width = qkv_w.shape[0]
        groups = qkv_w.shape[1]
        hidden_width = gu_w.shape[2]
        segment_row = segments[number]
        rows_in = layer_input[number]
        normed_attn, scale_attn = norm_forward(rows_in, g_attn)
        gathered_attn = spread_forward(normed_attn)
        row_count = gathered_attn.shape[0]
        qkv_rows = jnp.dot(
            gathered_attn, qkv_w.reshape(model_width, -1), preferred_element_type=jnp.float32
        ).reshape(row_count, groups, -1)
        mixed, saved = attend_forward(qkv_rows, segment_row, head_group, HD)

        def attn_term(row_start, row_span):
            return right_product(mixed, out_w)

        residual = rows_in + branch_sum(attn_term, local_rows)
        normed_mlp, scale_mlp = norm_forward(residual, g_mlp)
        gathered_mlp = spread_forward(normed_mlp)
        gate_up = jnp.dot(
            gathered_mlp, gu_w.reshape(model_width, -1), preferred_element_type=jnp.float32
        ).reshape(row_count, 2, hidden_width)
        gate_part = gate_up[:, 0]
        up_part = gate_up[:, 1]
        sigmoid_gate = jax.nn.sigmoid(gate_part)
        active = gate_part * sigmoid_gate
        hidden = (active * up_part).astype(jnp.bfloat16)

        def mlp_term(row_start, row_span):
            return right_product(hidden, down_w)

        outputs.append(residual + branch_sum(mlp_term, local_rows))
        back_weights = (
            lax.all_gather(weight_shard[0], "dp", axis=0, tiled=True),
            lax.all_gather(weight_shard[1], "dp", axis=0, tiled=True),
            lax.all_gather(weight_shard[2], "dp", axis=0, tiled=True),
            lax.all_gather(weight_shard[3], "dp", axis=0, tiled=True),
            lax.all_gather(weight_shard[4], "dp", axis=0, tiled=True),
            lax.all_gather(weight_shard[5], "dp", axis=0, tiled=True),
        )
        g_attn, qkv_w, out_w, g_mlp, gu_w, down_w = back_weights
        grad_in = cotangent[number]
        grad_rows = spread_backward(grad_in.astype(jnp.bfloat16))
        grad_down = outer_product(grad_rows, hidden)
        grad_hidden = jnp.dot(grad_rows, down_w, preferred_element_type=jnp.float32)
        grad_gu = jnp.stack(
            [
                grad_hidden * up_part * sigmoid_gate * (1.0 + gate_part * (1.0 - sigmoid_gate)),
                grad_hidden * active,
            ],
            axis=1,
        ).astype(jnp.bfloat16)
        flat_gu = grad_gu.reshape(row_count, -1)
        grad_gu_w = outer_product(gathered_mlp, flat_gu).reshape(model_width, 2, hidden_width)
        gu_flat = gu_w.reshape(model_width, -1)

        def mlp_back(row_start, row_span):
            return right_product(flat_gu, gu_flat)

        grad_normed_mlp = input_sum(mlp_back, local_rows)
        back_mlp, grad_g_mlp = norm_backward(residual, scale_mlp, g_mlp, grad_normed_mlp)
        grad_resid = grad_in + back_mlp
        resid_rows = spread_backward(grad_resid.astype(jnp.bfloat16))
        grad_out_w = outer_product(resid_rows, mixed)
        grad_mixed = jnp.dot(resid_rows, out_w, preferred_element_type=jnp.float32).astype(
            jnp.bfloat16
        )
        grad_qkv = attend_backward(grad_mixed, saved, HD)
        flat_qkv = grad_qkv.reshape(row_count, -1)
        grad_qkv_w = outer_product(gathered_attn, flat_qkv).reshape(qkv_w.shape)
        qkv_flat = qkv_w.reshape(model_width, -1)

        def attn_back(row_start, row_span):
            return right_product(flat_qkv, qkv_flat)

        grad_normed_attn = input_sum(attn_back, local_rows)
        back_attn, grad_g_attn = norm_backward(rows_in, scale_attn, g_attn, grad_normed_attn)
        input_grads.append(grad_resid + back_attn)
        grad_terms = (grad_g_attn, grad_qkv_w, grad_out_w, grad_g_mlp, grad_gu_w, grad_down)
        grad_total = add_terms(grad_total, grad_terms)
    owned_grads = lax.psum_scatter(grad_total, "dp", scatter_dimension=0, tiled=True)
    gain_first, gain_second = lax.psum((owned_grads[0], owned_grads[3]), "tensor")
    return (
        jnp.stack(outputs),
        jnp.stack(input_grads),
        gain_first,
        owned_grads[1],
        owned_grads[2],
        gain_second,
        owned_grads[4],
        owned_grads[5],
    )


def solution(mesh):
    placed = (
        P("dp", "tensor", None),
        P("dp", None),
        P("dp"),
        P("dp", "tensor", None),
        P("dp", "tensor"),
        P("dp"),
        P("dp", None, "tensor"),
        P("dp", "tensor"),
        P("dp", "tensor", None),
    )
    return jax.shard_map(
        body,
        mesh=mesh,
        in_specs=placed,
        out_specs=(
            P("dp", "tensor", None),
            P("dp", "tensor", None),
            P("dp"),
            P("dp", "tensor", None),
            P("dp", "tensor"),
            P("dp"),
            P("dp", None, "tensor"),
            P("dp", "tensor"),
        ),
        check_vma=False,
    )
```

profile of v0, /device:TPU:0, one launch (start us, length us, event | category | flops | bytes accessed | tf_op | source)
XLA Modules:
  0.0 1613.4 jit_solution(4839132049116461535)
XLA Ops:
  26.1 42.1 %all-gather.15.cloned.1.call-done = bf16[512,2048]{1,0:T(8,128)(2,1)} async-done(((bf16[128,2048]{1,0:T(8,128)(2,1)}), bf16[512,2048]{1,0:T(8,128)(2,1)}) %all-gather.15.cloned.1.call-update) | async-done | bytes 2097168 | tf_op jit(solution)/shard_map/all_gather | solution.py:158
  68.2 30.7 %all-gather.17.cloned.1.call-done = bf16[2048,1,640]{2,0,1:T(8,128)(2,1)} async-done(((bf16[256,1,640]{2,0,1:T(8,128)(2,1)}), bf16[2048,1,640]{2,0,1:T(8,128)(2,1)}) %all-gather.17.cloned.1.call-update) | async-done | bytes 2621456 | tf_op jit(solution)/shard_map/all_gather | solution.py:202
  105.6 41.1 %all-gather.27.cloned.1.call-done = bf16[512,2048]{1,0:T(8,128)(2,1)} async-done(((bf16[128,2048]{1,0:T(8,128)(2,1)}), bf16[512,2048]{1,0:T(8,128)(2,1)}) %all-gather.27.cloned.1.call-update) | async-done | bytes 2097168 | tf_op jit(solution)/shard_map/all_gather | solution.py:158
  210.8 46.2 %reduce-scatter.13.cloned.1.call-done = f32[128,2048]{1,0:T(8,128)} async-done(((f32[512,2048]{1,0:T(8,128)}), f32[128,2048]{1,0:T(8,128)}) %reduce-scatter.13.cloned.1.call-update) | async-done | bytes 1048592 | tf_op jit(solution)/shard_map/reduce_scatter | solution.py:166
  257.0 79.5 %reduce-scatter.17.cloned.1.call-done = f32[128,2048]{1,0:T(8,128)} async-done(((f32[512,2048]{1,0:T(8,128)}), f32[128,2048]{1,0:T(8,128)}) %reduce-scatter.17.cloned.1.call-update) | async-done | bytes 1048592 | tf_op jit(solution)/shard_map/reduce_scatter | solution.py:166
  343.9 63.1 %all-gather.23.cloned.1.call-done = bf16[2048,2,1408]{2,0,1:T(8,128)(2,1)} async-done(((bf16[256,2,1408]{2,0,1:T(8,128)(2,1)}), bf16[2048,2,1408]{2,0,1:T(8,128)(2,1)}) %all-gather.23.cloned.1.call-update) | async-done | bytes 11534352 | tf_op jit(solution)/shard_map/all_gather | solution.py:205
  422.2 32.6 %all-gather.21.cloned.1.call-done = bf16[512,2048]{1,0:T(8,128)(2,1)} async-done(((bf16[128,2048]{1,0:T(8,128)(2,1)}), bf16[512,2048]{1,0:T(8,128)(2,1)}) %all-gather.21.cloned.1.call-update) | async-done | bytes 2097168 | tf_op jit(solution)/shard_map/all_gather | solution.py:158
  466.6 34.8 %all-gather.31.cloned.1.call-done = bf16[512,2048]{1,0:T(8,128)(2,1)} async-done(((bf16[128,2048]{1,0:T(8,128)(2,1)}), bf16[512,2048]{1,0:T(8,128)(2,1)}) %all-gather.31.cloned.1.call-update) | async-done | bytes 2097168 | tf_op jit(solution)/shard_map/all_gather | solution.py:162
  501.5 43.8 %all-gather.25.cloned.1.call-done = bf16[2048,1408]{1,0:T(8,128)(2,1)} async-done(((bf16[256,1408]{1,0:T(8,128)(2,1)}), bf16[2048,1408]{1,0:T(8,128)(2,1)}) %all-gather.25.cloned.1.call-update) | async-done | bytes 5767184 | tf_op jit(solution)/shard_map/all_gather | solution.py:206
  566.2 76.9 %reduce-scatter.21.cloned.1.call-done = f32[128,2048]{1,0:T(8,128)} async-done(((f32[512,2048]{1,0:T(8,128)}), f32[128,2048]{1,0:T(8,128)}) %reduce-scatter.21.cloned.1.call-update) | async-done | bytes 1048592 | tf_op jit(solution)/shard_map/reduce_scatter | solution.py:175
  647.0 45.4 %all-gather.29.cloned.1.call-done = bf16[512,2048]{1,0:T(8,128)(2,1)} async-done(((bf16[128,2048]{1,0:T(8,128)(2,1)}), bf16[512,2048]{1,0:T(8,128)(2,1)}) %all-gather.29.cloned.1.call-update) | async-done | bytes 2097168 | tf_op jit(solution)/shard_map/all_gather | solution.py:158
  704.2 34.9 %all-gather.35.cloned.1.call-done = bf16[512,2048]{1,0:T(8,128)(2,1)} async-done(((bf16[128,2048]{1,0:T(8,128)(2,1)}), bf16[512,2048]{1,0:T(8,128)(2,1)}) %all-gather.35.cloned.1.call-update) | async-done | bytes 2097168 | tf_op jit(solution)/shard_map/all_gather | solution.py:162
  785.5 50.3 %reduce-scatter.25.cloned.1.call-done = f32[128,2048]{1,0:T(8,128)} async-done(((f32[512,2048]{1,0:T(8,128)}), f32[128,2048]{1,0:T(8,128)}) %reduce-scatter.25.cloned.1.call-update) | async-done | bytes 1048592 | tf_op jit(solution)/shard_map/reduce_scatter | solution.py:175
  837.3 78.0 %reduce-scatter.15.cloned.1.call-done = f32[128,2048]{1,0:T(8,128)} async-done(((f32[512,2048]{1,0:T(8,128)}), f32[128,2048]{1,0:T(8,128)}) %reduce-scatter.15.cloned.1.call-update) | async-done | bytes 1048592 | tf_op jit(solution)/shard_map/reduce_scatter | solution.py:166
  915.2 79.5 %reduce-scatter.19.cloned.1.call-done = f32[128,2048]{1,0:T(8,128)} async-done(((f32[512,2048]{1,0:T(8,128)}), f32[128,2048]{1,0:T(8,128)}) %reduce-scatter.19.cloned.1.call-update) | async-done | bytes 1048592 | tf_op jit(solution)/shard_map/reduce_scatter | solution.py:166
  1012.7 33.7 %all-gather.33.cloned.1.call-done = bf16[512,2048]{1,0:T(8,128)(2,1)} async-done(((bf16[128,2048]{1,0:T(8,128)(2,1)}), bf16[512,2048]{1,0:T(8,128)(2,1)}) %all-gather.33.cloned.1.call-update) | async-done | bytes 2097168 | tf_op jit(solution)/shard_map/all_gather | solution.py:162
  1061.9 31.0 %all-gather.37.cloned.1.call-done = bf16[512,2048]{1,0:T(8,128)(2,1)} async-done(((bf16[128,2048]{1,0:T(8,128)(2,1)}), bf16[512,2048]{1,0:T(8,128)(2,1)}) %all-gather.37.cloned.1.call-update) | async-done | bytes 2097168 | tf_op jit(solution)/shard_map/all_gather | solution.py:162
  1161.7 17.7 %convolution_add_fusion = f32[2048,2,1408]{2,0,1:T(8,128)} fusion(f32[2048,2,1408]{2,0,1:T(8,128)} %fusion.21, bf16[512,2,1408]{0,2,1:T(8,128)(2,1)} %copy.110, bf16[512,2048]{1,0:T(8,128)(2,1)} %all-gather.29.cloned.1.call-done), kind=kOutput, calls=%fused_computation | convolution fusion | flops 5911347200 | bytes 51118080 | tf_op jit(solution)/shard_map/dot_general | solution.py:146
  1193.3 48.5 %reduce-scatter.29.cloned.1.call-done = f32[256,1,640]{2,0,1:T(8,128)} async-done(((f32[2048,1,640]{2,0,1:T(8,128)}), f32[256,1,640]{2,0,1:T(8,128)}) %reduce-scatter.29.cloned.1.call-update) | async-done | bytes 655376 | tf_op jit(solution)/shard_map/reduce_scatter | solution.py:289
  1244.4 76.5 %reduce-scatter.27.cloned.1.call-done = f32[128,2048]{1,0:T(8,128)} async-done(((f32[512,2048]{1,0:T(8,128)}), f32[128,2048]{1,0:T(8,128)}) %reduce-scatter.27.cloned.1.call-update) | async-done | bytes 1048592 | tf_op jit(solution)/shard_map/reduce_scatter | solution.py:175
  1320.9 79.6 %reduce-scatter.23.cloned.1.call-done = f32[128,2048]{1,0:T(8,128)} async-done(((f32[512,2048]{1,0:T(8,128)}), f32[128,2048]{1,0:T(8,128)}) %reduce-scatter.23.cloned.1.call-update) | async-done | bytes 1048592 | tf_op jit(solution)/shard_map/reduce_scatter | solution.py:175
  1402.7 23.7 %all-reduce.2 = (f32[2048]{0:T(1024)S(1)}, f32[2048]{0:T(1024)S(1)}) all-reduce(f32[2048]{0:T(1024)S(1)} %add.202, f32[2048]{0:T(1024)S(1)} %add.206), channel_id=10, replica_groups=mesh['dp'=8,'tensor'=4] {'dp'}, use_global_device_ids=true, to_apply=%region_26.27.clone | all-reduce | flops 4096 | bytes 32768
  1442.4 108.7 %reduce-scatter.33.cloned.1.call-done = f32[256,2,1408]{2,0,1:T(8,128)} async-done(((f32[2048,2,1408]{2,0,1:T(8,128)}), f32[256,2,1408]{2,0,1:T(8,128)}) %reduce-scatter.33.cloned.1.call-update) | async-done | bytes 2883600 | tf_op jit(solution)/shard_map/reduce_scatter | solution.py:289
  1556.7 49.4 %reduce-scatter.31.cloned.1.call-done = f32[256,512]{1,0:T(8,128)} async-done(((f32[2048,512]{1,0:T(8,128)}), f32[256,512]{1,0:T(8,128)}) %reduce-scatter.31.cloned.1.call-update) | async-done | bytes 524304 | tf_op jit(solution)/shard_map/reduce_scatter | solution.py:289
  (349 shorter events, 349.1 us)
Async XLA Ops:
  7.2 61.0 %all-gather.15.cloned.1.call-start = ((), (), s32[]{:S(2)}) async-start(), calls=%async_computation.12 | async-start | bytes 2621440 | tf_op jit(solution)/shard_map/all_gather | solution.py:158
  22.1 76.8 %all-gather.17.cloned.1.call-start = ((), (), s32[]{:S(2)}) async-start(), calls=%async_computation.13 | async-start | bytes 2949120 | tf_op jit(solution)/shard_map/all_gather | solution.py:202
  22.9 123.9 %all-gather.27.cloned.1.call-start = ((), (), s32[]{:S(2)}) async-start(), calls=%async_computation.20 | async-start | bytes 2621440 | tf_op jit(solution)/shard_map/all_gather | solution.py:158
  23.6 151.5 %all-gather.19.cloned.1.call-start = ((), (), s32[]{:S(2)}) async-start(), calls=%async_computation.14 | async-start | bytes 2359296 | tf_op jit(solution)/shard_map/all_gather | solution.py:203
  24.2 232.8 %reduce-scatter.13.cloned.1.call-start = ((), (), s32[]{:S(2)}) async-start(), calls=%async_computation.15 | async-start | bytes 5242880 | tf_op jit(solution)/shard_map/reduce_scatter | solution.py:166
  180.0 156.4 %reduce-scatter.17.cloned.1.call-start = ((), (), s32[]{:S(2)}) async-start(), calls=%async_computation.21 | async-start | bytes 5242880 | tf_op jit(solution)/shard_map/reduce_scatter | solution.py:166
  199.1 207.9 %all-gather.23.cloned.1.call-start = ((), (), s32[]{:S(2)}) async-start(), calls=%async_computation.17 | async-start | bytes 12976128 | tf_op jit(solution)/shard_map/all_gather | solution.py:205
  201.8 253.0 %all-gather.21.cloned.1.call-start = ((), (), s32[]{:S(2)}) async-start(), calls=%async_computation.16 | async-start | bytes 2621440 | tf_op jit(solution)/shard_map/all_gather | solution.py:158
  340.2 161.3 %all-gather.31.cloned.1.call-start = ((), (), s32[]{:S(2)}) async-start(), calls=%async_computation.24 | async-start | bytes 2621440 | tf_op jit(solution)/shard_map/all_gather | solution.py:162
  342.9 202.4 %all-gather.25.cloned.1.call-start = ((), (), s32[]{:S(2)}) async-start(), calls=%async_computation.18 | async-start | bytes 6488064 | tf_op jit(solution)/shard_map/all_gather | solution.py:206
  343.5 299.6 %reduce-scatter.21.cloned.1.call-start = ((), (), s32[]{:S(2)}) async-start(), calls=%async_computation.25 | async-start | bytes 5242880 | tf_op jit(solution)/shard_map/reduce_scatter | solution.py:175
  566.1 126.3 %all-gather.29.cloned.1.call-start = ((), (), s32[]{:S(2)}) async-start(), calls=%async_computation.22 | async-start | bytes 2621440 | tf_op jit(solution)/shard_map/all_gather | solution.py:158
  646.1 93.0 %all-gather.35.cloned.1.call-start = ((), (), s32[]{:S(2)}) async-start(), calls=%async_computation.28 | async-start | bytes 2621440 | tf_op jit(solution)/shard_map/all_gather | solution.py:162
  646.8 188.9 %reduce-scatter.25.cloned.1.call-start = ((), (), s32[]{:S(2)}) async-start(), calls=%async_computation.29 | async-start | bytes 5242880 | tf_op jit(solution)/shard_map/reduce_scatter | solution.py:175
  760.0 155.2 %reduce-scatter.15.cloned.1.call-start = ((), (), s32[]{:S(2)}) async-start(), calls=%async_computation.19 | async-start | bytes 5242880 | tf_op jit(solution)/shard_map/reduce_scatter | solution.py:166
  772.7 222.0 %reduce-scatter.19.cloned.1.call-start = ((), (), s32[]{:S(2)}) async-start(), calls=%async_computation.23 | async-start | bytes 5242880 | tf_op jit(solution)/shard_map/reduce_scatter | solution.py:166
  785.4 261.0 %all-gather.33.cloned.1.call-start = ((), (), s32[]{:S(2)}) async-start(), calls=%async_computation.26 | async-start | bytes 2621440 | tf_op jit(solution)/shard_map/all_gather | solution.py:162
  1000.1 92.8 %all-gather.37.cloned.1.call-start = ((), (), s32[]{:S(2)}) async-start(), calls=%async_computation.30 | async-start | bytes 2621440 | tf_op jit(solution)/shard_map/all_gather | solution.py:162
  1000.7 189.6 %reduce-scatter.35.cloned.1.call-start = ((), (), s32[]{:S(2)}) async-start(), calls=%async_computation.35 | async-start | bytes 12976128 | tf_op jit(solution)/shard_map/reduce_scatter | solution.py:289
  1012.2 229.6 %reduce-scatter.29.cloned.1.call-start = ((), (), s32[]{:S(2)}) async-start(), calls=%async_computation.32 | async-start | bytes 5898240 | tf_op jit(solution)/shard_map/reduce_scatter | solution.py:289
  1128.9 192.0 %reduce-scatter.27.cloned.1.call-start = ((), (), s32[]{:S(2)}) async-start(), calls=%async_computation.31 | async-start | bytes 5242880 | tf_op jit(solution)/shard_map/reduce_scatter | solution.py:175
  1134.5 266.0 %reduce-scatter.23.cloned.1.call-start = ((), (), s32[]{:S(2)}) async-start(), calls=%async_computation.27 | async-start | bytes 5242880 | tf_op jit(solution)/shard_map/reduce_scatter | solution.py:175
  1140.4 410.7 %reduce-scatter.33.cloned.1.call-start = ((), (), s32[]{:S(2)}) async-start(), calls=%async_computation.34 | async-start | bytes 25952256 | tf_op jit(solution)/shard_map/reduce_scatter | solution.py:289
  1179.5 426.6 %reduce-scatter.31.cloned.1.call-start = ((), (), s32[]{:S(2)}) async-start(), calls=%async_computation.33 | async-start | bytes 4718592 | tf_op jit(solution)/shard_map/reduce_scatter | solution.py:289
  (94 other events, 2699.0 us)
Sparse Core Ops, SparseCore 0:
  22.2 45.9 all-gather.14
  70.1 28.7 all-gather.16
  101.1 45.6 all-gather.26
  148.5 26.5 all-gather.18
  180.1 76.7 reduce-scatter.12
  259.1 77.2 reduce-scatter.16
  338.9 68.0 all-gather.22
  409.2 45.6 all-gather.20
  457.0 44.4 all-gather.30
  503.2 41.9 all-gather.24
  566.3 76.7 reduce-scatter.20
  646.2 46.1 all-gather.28
  694.5 44.4 all-gather.34
  760.1 75.5 reduce-scatter.24
  837.9 77.2 reduce-scatter.14
  917.4 77.2 reduce-scatter.18
  1000.2 46.1 all-gather.32
  1048.4 44.4 all-gather.36
  1096.4 85.6 reduce-scatter.34
  1185.3 56.4 reduce-scatter.28
  1244.1 76.7 reduce-scatter.26
  1323.2 77.2 reduce-scatter.22
  1404.2 146.8 reduce-scatter.32
  1554.9 51.1 reduce-scatter.30
where the time goes:
time: 1620 us; the launch traced here: 1610 us
  waiting for transfers between devices  1220 us (75%)
  matrix products  200 us (12%)
  local copies, waits for them, and re-layouts  62.7 us (4%)
  blocking collectives  55 us (3%)
  other arithmetic  52.8 us (3%)
  between operations  16.8 us (1%)
    reduce_scatter x4, waiting for transfers between devices, input_sum(): lax.psum_scatter(term_fn(jnp.int32(0), lax.axis_size('tensor') * local_ro...  283 us
    reduce_scatter x4, waiting for transfers between devices, branch_sum(): lax.psum_scatter(term_fn(jnp.int32(0), lax.axis_size('tensor') * local_ro...  283 us
    reduce_scatter x4, waiting for transfers between devices, body(): lax.psum_scatter(grad_total, 'dp', scatter_dimension=0, tiled=True)  207 us
    all_gather x4, waiting for transfers between devices, spread_forward(): return lax.all_gather(row_block, 'tensor', axis=0, tiled=True)  161 us
    all_gather x4, waiting for transfers between devices, spread_backward(): return lax.all_gather(row_block, 'tensor', axis=0, tiled=True)  134 us
    all_gather x1, waiting for transfers between devices, body(): lax.all_gather(weight_shard[4], 'dp', axis=0, tiled=True)  63.1 us
    dot_general x8, matrix products, right_product(): lax.dot_general(left_rows, right_matrix, (((1,), (1,)), ((), ())), prefer...  55.7 us
    dot_general x8, matrix products, outer_product(): lax.dot_general(left_rows, right_rows, (((0,), (0,)), ((), ())), preferre...  55.1 us
  transfers between devices with their start and end apart: 24, of which 23 were waited for; matrix products, arithmetic and copies ran while one was open for 15% of the time, Pallas kernels for 0%

commit v1 on v0

--- a/solution.py
+++ b/solution.py
@@ -8,6 +8,17 @@
 KV = 4
 HD = 64
 NORM_EPS = 1e-05
+
+
+def ring_gather(x, axis, dim):
+    ways = lax.axis_size(axis)
+    pieces = [x]
+    for far in range(1, ways):
+        pieces.append(
+            lax.ppermute(pieces[far - 1], axis, [(d, (d - 1) % ways) for d in range(ways)])
+        )
+    line = jnp.concatenate(pieces, axis=dim)
+    return jnp.roll(line, lax.axis_index(axis) * x.shape[dim], axis=dim)
 
 
 def rope_tables(segment_row, head_size):
@@ -155,7 +166,7 @@
 
 
 def spread_forward(row_block):
-    return lax.all_gather(row_block, "tensor", axis=0, tiled=True)
+    return ring_gather(row_block, "tensor", 0)
 
 
 def spread_backward(row_block):

time: 1620 us -> 1520 us (0.938)
  waiting for transfers between devices: 1220 us -> 1060 us
  starting transfers between devices: 2.85 us -> 41.2 us
  other arithmetic: 52.8 us -> 85.6 us
    all_gather x4 -> x0, waiting for transfers between devices: 161 us -> none  [spread_forward(): return lax.all_gather(row_block, 'tensor', axis=0, tiled=True)]
    ppermute x0 -> x12, waiting for transfers between devices: none -> 135 us  [ring_gather(): lax.ppermute(pieces[far - 1], axis, [(d, (d - 1) % ways) for d in range(w...]
    all_gather x4, waiting for transfers between devices: 134 us -> 86.6 us  [spread_backward(): return lax.all_gather(row_block, 'tensor', axis=0, tiled=True)]
    all_gather x1, waiting for transfers between devices: 63.1 us -> 16.4 us  [body(): lax.all_gather(weight_shard[4], 'dp', axis=0, tiled=True)]
    ppermute x0 -> x12, starting transfers between devices: none -> 39.8 us  [ring_gather(): lax.ppermute(pieces[far - 1], axis, [(d, (d - 1) % ways) for d in range(w...]
    all_gather x1, waiting for transfers between devices: 30.7 us -> 0.01 us  [body(): lax.all_gather(weight_shard[1], 'dp', axis=0, tiled=True)]
    concatenate x0 -> x2, other arithmetic: none -> 17 us  [ring_gather(): return jnp.roll(line, lax.axis_index(axis) * x.shape[dim], axis=dim)]
    dynamic_slice x0 -> x2, other arithmetic: none -> 16.8 us  [ring_gather(): return jnp.roll(line, lax.axis_index(axis) * x.shape[dim], axis=dim)]
  transfers between devices with their start and end apart: 24 -> 32, of which waited for: 23 -> 28; matrix products, arithmetic and copies ran while one was open for 15% -> 18% of each run, Pallas kernels for 0% -> 0%
where the time goes in v1:
time: 1520 us
  waiting for transfers between devices  1060 us (70%)
  matrix products  197 us (13%)
  other arithmetic  85.6 us (6%)
  local copies, waits for them, and re-layouts  61.7 us (4%)
  blocking collectives  55 us (4%)
  starting transfers between devices  41.2 us (3%)
  between operations  16.6 us (1%)
    reduce_scatter x4, waiting for transfers between devices, input_sum(): lax.psum_scatter(term_fn(jnp.int32(0), lax.axis_size('tensor') * local_ro...  287 us
    reduce_scatter x4, waiting for transfers between devices, branch_sum(): lax.psum_scatter(term_fn(jnp.int32(0), lax.axis_size('tensor') * local_ro...  286 us
    reduce_scatter x4, waiting for transfers between devices, body(): lax.psum_scatter(grad_total, 'dp', scatter_dimension=0, tiled=True)  203 us
    ppermute x12, waiting for transfers between devices, ring_gather(): lax.ppermute(pieces[far - 1], axis, [(d, (d - 1) % ways) for d in range(w...  135 us
    all_gather x4, waiting for transfers between devices, spread_backward(): return lax.all_gather(row_block, 'tensor', axis=0, tiled=True)  86.6 us
    dot_general x8, matrix products, right_product(): lax.dot_general(left_rows, right_matrix, (((1,), (1,)), ((), ())), prefer...  56 us
    dot_general x8, matrix products, outer_product(): lax.dot_general(left_rows, right_rows, (((0,), (0,)), ((), ())), preferre...  53.8 us
    all_gather x1, waiting for transfers between devices, body(): lax.all_gather(weight_shard[5], 'dp', axis=0, tiled=True)  43.9 us
  transfers between devices with their start and end apart: 32, of which 28 were waited for; matrix products, arithmetic and copies ran while one was open for 18% of the time, Pallas kernels for 0%

profile of v1, /device:TPU:0, one launch (start us, length us, event | category | flops | bytes accessed | tf_op | source)
XLA Modules:
  0.0 1517.0 jit_solution(17959786682666895539)
XLA Ops:
  158.5 48.4 %reduce-scatter.13.cloned.1.call-done = f32[128,2048]{1,0:T(8,128)} async-done(((f32[512,2048]{1,0:T(8,128)}), f32[128,2048]{1,0:T(8,128)}) %reduce-scatter.13.cloned.1.call-update) | async-done | bytes 1048592 | tf_op jit(solution)/shard_map/reduce_scatter | solution.py:177
  206.9 79.5 %reduce-scatter.17.cloned.1.call-done = f32[128,2048]{1,0:T(8,128)} async-done(((f32[512,2048]{1,0:T(8,128)}), f32[128,2048]{1,0:T(8,128)}) %reduce-scatter.17.cloned.1.call-update) | async-done | bytes 1048592 | tf_op jit(solution)/shard_map/reduce_scatter | solution.py:177
  340.5 16.4 %all-gather.15.cloned.1.call-done = bf16[2048,2,1408]{2,0,1:T(8,128)(2,1)} async-done(((bf16[256,2,1408]{2,0,1:T(8,128)(2,1)}), bf16[2048,2,1408]{2,0,1:T(8,128)(2,1)}) %all-gather.15.cloned.1.call-update) | async-done | bytes 11534352 | tf_op jit(solution)/shard_map/all_gather | solution.py:216
  356.8 15.2 %copy.87 = bf16[2048,2,1408]{0,2,1:T(8,128)(2,1)} copy(bf16[2048,2,1408]{2,0,1:T(8,128)(2,1)} %all-gather.15.cloned.1.call-done) | data formatting | bytes 23068672 | tf_op jit(solution)/shard_map/all_gather | solution.py:216
  383.2 21.3 %all-gather.19.cloned.1.call-done = bf16[512,2048]{1,0:T(8,128)(2,1)} async-done(((bf16[128,2048]{1,0:T(8,128)(2,1)}), bf16[512,2048]{1,0:T(8,128)(2,1)}) %all-gather.19.cloned.1.call-update) | async-done | bytes 2097168 | tf_op jit(solution)/shard_map/all_gather | solution.py:173
  404.5 43.9 %all-gather.17.cloned.1.call-done = bf16[2048,1408]{1,0:T(8,128)(2,1)} async-done(((bf16[256,1408]{1,0:T(8,128)(2,1)}), bf16[2048,1408]{1,0:T(8,128)(2,1)}) %all-gather.17.cloned.1.call-update) | async-done | bytes 5767184 | tf_op jit(solution)/shard_map/all_gather | solution.py:217
  469.8 76.9 %reduce-scatter.21.cloned.1.call-done = f32[128,2048]{1,0:T(8,128)} async-done(((f32[512,2048]{1,0:T(8,128)}), f32[128,2048]{1,0:T(8,128)}) %reduce-scatter.21.cloned.1.call-update) | async-done | bytes 1048592 | tf_op jit(solution)/shard_map/reduce_scatter | solution.py:186
  551.6 15.8 %collective-permute-done.9 = bf16[128,2048]{1,0:T(8,128)(2,1)S(1)} collective-permute-done((bf16[128,2048]{1,0:T(8,128)(2,1)S(1)}, bf16[128,2048]{1,0:T(8,128)(2,1)S(1)}, u32[]{:S(2)}, u32[]{:S(2)}) %collective-permute-start.9) | collective-permute-done | bytes 524320 | tf_op jit(solution)/shard_map/ppermute | solution.py:18
  571.7 34.4 %collective-permute-done.10 = bf16[128,2048]{1,0:T(8,128)(2,1)S(1)} collective-permute-done((bf16[128,2048]{1,0:T(8,128)(2,1)S(1)}, bf16[128,2048]{1,0:T(8,128)(2,1)S(1)}, u32[]{:S(2)}, u32[]{:S(2)}) %collective-permute-start.10) | collective-permute-done | bytes 524320 | tf_op jit(solution)/shard_map/ppermute | solution.py:18
  606.1 13.1 collective-permute-done.11
  685.8 54.0 %reduce-scatter.25.cloned.1.call-done = f32[128,2048]{1,0:T(8,128)} async-done(((f32[512,2048]{1,0:T(8,128)}), f32[128,2048]{1,0:T(8,128)}) %reduce-scatter.25.cloned.1.call-update) | async-done | bytes 1048592 | tf_op jit(solution)/shard_map/reduce_scatter | solution.py:186
  741.3 78.1 %reduce-scatter.15.cloned.1.call-done = f32[128,2048]{1,0:T(8,128)} async-done(((f32[512,2048]{1,0:T(8,128)}), f32[128,2048]{1,0:T(8,128)}) %reduce-scatter.15.cloned.1.call-update) | async-done | bytes 1048592 | tf_op jit(solution)/shard_map/reduce_scatter | solution.py:177
  819.4 79.5 %reduce-scatter.19.cloned.1.call-done = f32[128,2048]{1,0:T(8,128)} async-done(((f32[512,2048]{1,0:T(8,128)}), f32[128,2048]{1,0:T(8,128)}) %reduce-scatter.19.cloned.1.call-update) | async-done | bytes 1048592 | tf_op jit(solution)/shard_map/reduce_scatter | solution.py:177
  916.6 34.0 %all-gather.21.cloned.1.call-done = bf16[512,2048]{1,0:T(8,128)(2,1)} async-done(((bf16[128,2048]{1,0:T(8,128)(2,1)}), bf16[512,2048]{1,0:T(8,128)(2,1)}) %all-gather.21.cloned.1.call-update) | async-done | bytes 2097168 | tf_op jit(solution)/shard_map/all_gather | solution.py:173
  965.9 31.2 %all-gather.25.cloned.1.call-done = bf16[512,2048]{1,0:T(8,128)(2,1)} async-done(((bf16[128,2048]{1,0:T(8,128)(2,1)}), bf16[512,2048]{1,0:T(8,128)(2,1)}) %all-gather.25.cloned.1.call-update) | async-done | bytes 2097168 | tf_op jit(solution)/shard_map/all_gather | solution.py:173
  1052.6 13.2 fusion.21
  1068.9 16.6 %convolution_add_fusion = f32[2048,2,1408]{2,0,1:T(8,128)} fusion(f32[2048,2,1408]{2,0,1:T(8,128)} %fusion.21, bf16[512,2048,1]{1,0,2:T(8,128)(2,1)} %copy-done.12, bf16[512,2,1408]{0,2,1:T(8,128)(2,1)} %copy.110), kind=kOutput, calls=%fused_computation | convolution fusion | flops 5911347200 | bytes 51118080 | tf_op jit(solution)/shard_map/dot_general | solution.py:157
  1100.8 45.2 %reduce-scatter.29.cloned.1.call-done = f32[256,1,640]{2,0,1:T(8,128)} async-done(((f32[2048,1,640]{2,0,1:T(8,128)}), f32[256,1,640]{2,0,1:T(8,128)}) %reduce-scatter.29.cloned.1.call-update) | async-done | bytes 655376 | tf_op jit(solution)/shard_map/reduce_scatter | solution.py:300
  1148.6 76.3 %reduce-scatter.23.cloned.1.call-done = f32[128,2048]{1,0:T(8,128)} async-done(((f32[512,2048]{1,0:T(8,128)}), f32[128,2048]{1,0:T(8,128)}) %reduce-scatter.23.cloned.1.call-update) | async-done | bytes 1048592 | tf_op jit(solution)/shard_map/reduce_scatter | solution.py:186
  1224.9 79.5 %reduce-scatter.27.cloned.1.call-done = f32[128,2048]{1,0:T(8,128)} async-done(((f32[512,2048]{1,0:T(8,128)}), f32[128,2048]{1,0:T(8,128)}) %reduce-scatter.27.cloned.1.call-update) | async-done | bytes 1048592 | tf_op jit(solution)/shard_map/reduce_scatter | solution.py:186
  1306.5 23.7 %all-reduce.2 = (f32[2048]{0:T(1024)S(1)}, f32[2048]{0:T(1024)S(1)}) all-reduce(f32[2048]{0:T(1024)S(1)} %add.210, f32[2048]{0:T(1024)S(1)} %add.214), channel_id=10, replica_groups=mesh['dp'=8,'tensor'=4] {'dp'}, use_global_device_ids=true, to_apply=%region_26.28.clone | all-reduce | flops 4096 | bytes 32768
  1330.4 12.0 all-reduce.3
  1346.2 108.7 %reduce-scatter.33.cloned.1.call-done = f32[256,2,1408]{2,0,1:T(8,128)} async-done(((f32[2048,2,1408]{2,0,1:T(8,128)}), f32[256,2,1408]{2,0,1:T(8,128)}) %reduce-scatter.33.cloned.1.call-update) | async-done | bytes 2883600 | tf_op jit(solution)/shard_map/reduce_scatter | solution.py:300
  1460.6 49.4 %reduce-scatter.31.cloned.1.call-done = f32[256,512]{1,0:T(8,128)} async-done(((f32[2048,512]{1,0:T(8,128)}), f32[256,512]{1,0:T(8,128)}) %reduce-scatter.31.cloned.1.call-update) | async-done | bytes 524304 | tf_op jit(solution)/shard_map/reduce_scatter | solution.py:300
  (376 shorter events, 433.9 us)
Async XLA Ops:
  7.2 97.0 %all-gather.11.cloned.1.call-start = ((), (), s32[]{:S(2)}) async-start(), calls=%async_computation.12 | async-start | bytes 2949120 | tf_op jit(solution)/shard_map/all_gather | solution.py:213
  7.9 116.0 %all-gather.13.cloned.1.call-start = ((), (), s32[]{:S(2)}) async-start(), calls=%async_computation.13 | async-start | bytes 2359296 | tf_op jit(solution)/shard_map/all_gather | solution.py:214
  27.0 23.5 %collective-permute-start.6 = (bf16[128,2048]{1,0:T(8,128)(2,1)S(1)}, bf16[128,2048]{1,0:T(8,128)(2,1)S(1)}, u32[]{:S(2)}, u32[]{:S(2)}) collective-permute-start(bf16[128,2048]{1,0:T(8,128)(2,1)S(1)} %get-tuple-element.66), channel_id=1, source_target_pairs={{0,3},{1,0},{2,1},{3,2},{4,7},{5,4},{6,5},{7,6},{8,11},{9,8},{10,9... | collective-permute-start | bytes 1572872 | tf_op jit(solution)/shard_map/ppermute | solution.py:18
  27.5 179.4 %reduce-scatter.13.cloned.1.call-start = ((), (), s32[]{:S(2)}) async-start(), calls=%async_computation.14 | async-start | bytes 5242880 | tf_op jit(solution)/shard_map/reduce_scatter | solution.py:177
  39.3 22.5 %collective-permute-start.1 = (bf16[128,2048]{1,0:T(8,128)(2,1)S(1)}, bf16[128,2048]{1,0:T(8,128)(2,1)S(1)}, u32[]{:S(2)}, u32[]{:S(2)}) collective-permute-start(bf16[128,2048]{1,0:T(8,128)(2,1)S(1)} %collective-permute-done), channel_id=1, source_target_pairs={{0,3},{1,0},{2,1},{3,2},{4,7},{5,4},{6,5},{7,6},{8,11},{9,8},{10,9... | collective-permute-start | bytes 1572872 | tf_op jit(solution)/shard_map/ppermute | solution.py:18
  50.5 22.5 %collective-permute-start.7 = (bf16[128,2048]{1,0:T(8,128)(2,1)S(1)}, bf16[128,2048]{1,0:T(8,128)(2,1)S(1)}, u32[]{:S(2)}, u32[]{:S(2)}) collective-permute-start(bf16[128,2048]{1,0:T(8,128)(2,1)S(1)} %collective-permute-done.6), channel_id=1, source_target_pairs={{0,3},{1,0},{2,1},{3,2},{4,7},{5,4},{6,5},{7,6},{8,11},{9,8},{10,9... | collective-permute-start | bytes 1572872 | tf_op jit(solution)/shard_map/ppermute | solution.py:18
  129.0 157.4 %reduce-scatter.17.cloned.1.call-start = ((), (), s32[]{:S(2)}) async-start(), calls=%async_computation.18 | async-start | bytes 5242880 | tf_op jit(solution)/shard_map/reduce_scatter | solution.py:177
  143.4 213.4 %all-gather.15.cloned.1.call-start = ((), (), s32[]{:S(2)}) async-start(), calls=%async_computation.15 | async-start | bytes 12976128 | tf_op jit(solution)/shard_map/all_gather | solution.py:216
  146.0 258.5 %all-gather.19.cloned.1.call-start = ((), (), s32[]{:S(2)}) async-start(), calls=%async_computation.20 | async-start | bytes 2621440 | tf_op jit(solution)/shard_map/all_gather | solution.py:173
  148.7 299.7 %all-gather.17.cloned.1.call-start = ((), (), s32[]{:S(2)}) async-start(), calls=%async_computation.16 | async-start | bytes 6488064 | tf_op jit(solution)/shard_map/all_gather | solution.py:217
  149.5 397.2 %reduce-scatter.21.cloned.1.call-start = ((), (), s32[]{:S(2)}) async-start(), calls=%async_computation.21 | async-start | bytes 5242880 | tf_op jit(solution)/shard_map/reduce_scatter | solution.py:186
  469.7 170.2 %all-gather.23.cloned.1.call-start = ((), (), s32[]{:S(2)}) async-start(), calls=%async_computation.24 | async-start | bytes 2621440 | tf_op jit(solution)/shard_map/all_gather | solution.py:173
  551.5 188.3 %reduce-scatter.25.cloned.1.call-start = ((), (), s32[]{:S(2)}) async-start(), calls=%async_computation.25 | async-start | bytes 5242880 | tf_op jit(solution)/shard_map/reduce_scatter | solution.py:186
  567.4 38.7 %collective-permute-start.10 = (bf16[128,2048]{1,0:T(8,128)(2,1)S(1)}, bf16[128,2048]{1,0:T(8,128)(2,1)S(1)}, u32[]{:S(2)}, u32[]{:S(2)}) collective-permute-start(bf16[128,2048]{1,0:T(8,128)(2,1)S(1)} %collective-permute-done.9), channel_id=1, source_target_pairs={{0,3},{1,0},{2,1},{3,2},{4,7},{5,4},{6,5},{7,6},{8,11},{9,8},{10,9... | collective-permute-start | bytes 1572872 | tf_op jit(solution)/shard_map/ppermute | solution.py:18
  661.0 158.4 %reduce-scatter.15.cloned.1.call-start = ((), (), s32[]{:S(2)}) async-start(), calls=%async_computation.17 | async-start | bytes 5242880 | tf_op jit(solution)/shard_map/reduce_scatter | solution.py:177
  673.3 225.6 %reduce-scatter.19.cloned.1.call-start = ((), (), s32[]{:S(2)}) async-start(), calls=%async_computation.19 | async-start | bytes 5242880 | tf_op jit(solution)/shard_map/reduce_scatter | solution.py:177
  685.7 264.9 %all-gather.21.cloned.1.call-start = ((), (), s32[]{:S(2)}) async-start(), calls=%async_computation.22 | async-start | bytes 2621440 | tf_op jit(solution)/shard_map/all_gather | solution.py:173
  904.3 92.8 %all-gather.25.cloned.1.call-start = ((), (), s32[]{:S(2)}) async-start(), calls=%async_computation.26 | async-start | bytes 2621440 | tf_op jit(solution)/shard_map/all_gather | solution.py:173
  904.9 192.8 %reduce-scatter.35.cloned.1.call-start = ((), (), s32[]{:S(2)}) async-start(), calls=%async_computation.31 | async-start | bytes 12976128 | tf_op jit(solution)/shard_map/reduce_scatter | solution.py:300
  916.6 229.4 %reduce-scatter.29.cloned.1.call-start = ((), (), s32[]{:S(2)}) async-start(), calls=%async_computation.28 | async-start | bytes 5898240 | tf_op jit(solution)/shard_map/reduce_scatter | solution.py:300
  1036.1 188.9 %reduce-scatter.23.cloned.1.call-start = ((), (), s32[]{:S(2)}) async-start(), calls=%async_computation.23 | async-start | bytes 5242880 | tf_op jit(solution)/shard_map/reduce_scatter | solution.py:186
  1041.7 262.8 %reduce-scatter.27.cloned.1.call-start = ((), (), s32[]{:S(2)}) async-start(), calls=%async_computation.27 | async-start | bytes 5242880 | tf_op jit(solution)/shard_map/reduce_scatter | solution.py:186
  1047.7 407.2 %reduce-scatter.33.cloned.1.call-start = ((), (), s32[]{:S(2)}) async-start(), calls=%async_computation.30 | async-start | bytes 25952256 | tf_op jit(solution)/shard_map/reduce_scatter | solution.py:300
  1085.5 424.4 %reduce-scatter.31.cloned.1.call-start = ((), (), s32[]{:S(2)}) async-start(), calls=%async_computation.29 | async-start | bytes 4718592 | tf_op jit(solution)/shard_map/reduce_scatter | solution.py:300
  (108 other events, 3026.9 us)
Sparse Core Ops, SparseCore 0:
  9.9 32.6 all-gather.10
  44.5 27.7 all-gather.12
  129.1 77.7 reduce-scatter.12
  209.1 77.3 reduce-scatter.16
  288.7 68.0 all-gather.14
  358.8 45.6 all-gather.18
  406.4 41.9 all-gather.16
  469.9 76.7 reduce-scatter.20
  551.6 60.6 all-gather.22
  661.1 78.6 reduce-scatter.24
  742.1 77.2 reduce-scatter.14
  821.6 77.2 reduce-scatter.18
  904.4 46.1 all-gather.20
  952.6 44.4 all-gather.24
  1000.5 85.6 reduce-scatter.34
  1089.4 56.5 reduce-scatter.28
  1148.1 76.7 reduce-scatter.22
  1227.1 77.2 reduce-scatter.26
  1308.0 146.8 reduce-scatter.32
  1458.7 51.1 reduce-scatter.30
